TPU v7x, 32 devices: a whole 2x2x4 slice. The times are simulated.
32 devices in a mesh: row: 4 (over z), col: 8 (over y, x, core).
Axes of the slice: x: 2, y: 2, z: 4, core: 2. Of those that a mesh axis runs over, the one named last changes fastest.
Arguments:
- tile_values: bfloat16 [4, 8, 128, 128, 128], P('row', 'col'), may hold values from -0.1875 to 0.1875
- tile_rows: int32 [4, 8, 128], P('row', 'col'), may hold values from 0 to 15, as said below
- tile_cols: int32 [4, 8, 128], P('row', 'col'), may hold values from 0 to 15, as said below
- tile_count: int32 [4, 8], P('row', 'col'), may hold values from 42 to 128, as said below
- sinogram: float32 [8192, 128], P('row'), may hold values from -6 to 6
Outputs:
- solution: float32 [16384, 128], P('col')
- residual_estimate: float32 [128], replicated
Inputs may be any that keep to these rules, and one draw needn't show every extreme that they name: On each device the 128 slots name distinct tile positions (tile_rows, tile_cols) of its grid of 16 x 16 tiles. `tile_cols`: see tile_rows. `tile_count`: some device holds 128 tiles in every draw.
All inputs are finite; a program needn't handle non-finite values.
Results may differ from a plain program's by a relative error of at most 0.0019.
Values may be sent and summed in bfloat16 or wider, within the bound.
A program may use at most 128 MiB of HBM per device.

v0:
```python
import functools

import jax
import jax.numpy as jnp
from jax import lax
from jax.experimental import pallas as pl
from jax.experimental.pallas import tpu as pltpu
from jax.sharding import PartitionSpec as P

TC = 16
ITERS = 3
EPSILON = 1e-06
PAD = 16
TOP = 32000.0
MESH = pl.DeviceIdType.MESH


def pack(val):
    top = jnp.max(jnp.abs(val), axis=0, keepdims=True)
    exponent = jnp.ceil(jnp.log2(jnp.maximum(top, 1e-30)))
    scale = TOP * jnp.exp2(-exponent)
    coded = jnp.round(jnp.clip(val * scale, -32767.0, 32767.0))
    coded = coded.astype(jnp.int32).astype(jnp.int16)
    rows = jnp.broadcast_to(exponent, (PAD, val.shape[1]))
    return coded, rows.astype(jnp.int32).astype(jnp.int16)


def store_packet(ref, val):
    n = val.shape[0]
    coded, rows = pack(val)
    ref[pl.ds(0, n), :] = coded
    ref[pl.ds(n, PAD), :] = rows


def load_packet(ref):
    n = ref.shape[0] - PAD
    exponent = ref[pl.ds(n, PAD), :].astype(jnp.int32).astype(jnp.float32)[:1]
    scale = jnp.exp2(exponent) * (1.0 / TOP)
    return ref[pl.ds(0, n), :].astype(jnp.int32).astype(jnp.float32) * scale


def dot(a, b):
    return jnp.dot(a, b, preferred_element_type=jnp.float32)


def root(total_of):
    return jnp.sqrt(total_of() + EPSILON)


def squares(vec):
    return jnp.sum(vec * vec, axis=0, keepdims=True)


def kernel(
    nr, nc, inv, tiles, sino, sol, res,
    facc, bacc, sq, fa, ba, ybf, xbf, ray, vox, vfull, sdir,
    bsend, brecv, vgat, dsend, drecv, fsend, frecv, rgat, nrow, ncol, nlast,
    bs, br, vs, vr, ds_, dr, fs, fr, gs, gr, hs, hr, rs, rr, cs, cr, ls, lr,
):
    mr = lax.axis_index("row")
    mc = lax.axis_index("col")
    nch = nc // 2
    chip = mc // 2
    core = mc % 2
    partner = chip * 2 + (1 - core)
    tile = tiles.shape[1]
    mb, z = sino.shape
    nb = sol.shape[0]
    tr, tc = mb // tile, nb // tile
    sv, sr = nb // nr, mb // nc

    barrier = pltpu.get_barrier_semaphore()
    for s in range(1, nr):
        pl.semaphore_signal(barrier, 1, device_id=(lax.rem(mr + s, nr), mc), device_id_type=MESH)
    for s in range(1, nc):
        pl.semaphore_signal(barrier, 1, device_id=(mr, lax.rem(mc + s, nc)), device_id_type=MESH)

    def send(src, dst, ssem, rsem, row, col):
        copy = pltpu.make_async_remote_copy(
            src_ref=src, dst_ref=dst, send_sem=ssem, recv_sem=rsem,
            device_id=(row, col), device_id_type=MESH)
        copy.start()
        sent.append(copy)
        return copy

    sent = []

    def pick(i, j):
        slot = inv[i * tc + j]
        block = tiles[jnp.maximum(slot, 0)]
        return jnp.where(slot >= 0, block, jnp.zeros_like(block))

    @pl.loop(0, tc)
    def _(j):
        first = pl.multiple_of(j * tile, tile)
        for i in range(tr):
            ba[pl.ds(first, tile), i * tile:(i + 1) * tile] = pick(i, j).T

    def share(vec, buf, n, me, ssem, rsem, over_row):
        buf[me] = jnp.broadcast_to(vec, (8, z))
        copies = []
        for s in range(1, n):
            peer = lax.rem(me + s, n)
            place = (peer, mc) if over_row else (mr, peer)
            copies.append(send(buf.at[me], buf.at[me], ssem.at[s], rsem.at[s], *place))

        def finish():
            for copy in copies:
                copy.wait_recv()
            total = buf[0]
            for q in range(1, n):
                total = total + buf[q]
            return total[:1]

        return finish

    line = nr == 4
    inner = (mr == 1) | (mr == 2)
    left = mr < 2
    mate = mr + 1 - 2 * lax.rem(mr, 2)
    cross = jnp.where(left, 2, 1)
    far = jnp.where(left, 3, 0)
    early = jnp.where(inner, far, mate)
    late = jnp.where(inner, mate, far)
    inner_sent = []

    def row_copy(src, dst, ssem, rsem, row):
        return pltpu.make_async_remote_copy(
            src_ref=src, dst_ref=dst, send_sem=ssem, recv_sem=rsem,
            device_id=(row, mc), device_id_type=MESH)

    def back_part(k, dest):
        rows = pl.ds(pl.multiple_of(dest * sv, sv), sv)
        if k == 0:
            return dot(ba[rows, :], ybf[...])
        late = lax.rem(chip + 1, nch) * 2 * sr
        cols = pl.ds(pl.multiple_of(late, 2 * sr), 2 * sr)
        return bacc[rows, :] + dot(ba[rows, cols], ybf[cols, :])

    def back_arrived(k, slot):
        row_copy(bsend.at[k, slot], brecv.at[k, slot], bs.at[k, slot], br.at[k, slot], mate).wait_recv()

    def back_start(k):
        if line:
            store_packet(bsend.at[k, 0], back_part(k, jnp.where(inner, cross, far)))
            slot = jnp.where(inner, 3, 0)
            send(bsend.at[k, 0], brecv.at[k, slot], bs.at[k, 0], br.at[k, slot],
                 jnp.where(inner, cross, mate), mc)
            part = back_part(k, jnp.where(inner, far, cross))

            @pl.when(jnp.logical_not(inner))
            def _():
                store_packet(bsend.at[k, 1], part)

            @pl.when(inner)
            def _():
                back_arrived(k, 0)
                store_packet(bsend.at[k, 1], part + load_packet(brecv.at[k, 0]))

            send(bsend.at[k, 1], brecv.at[k, 1], bs.at[k, 1], br.at[k, 1], jnp.where(inner, far, cross), mc)
            store_packet(bsend.at[k, 2], back_part(k, mate))
            send(bsend.at[k, 2], brecv.at[k, 2], bs.at[k, 2], br.at[k, 2], mate, mc)
            vox[k] = back_part(k, mr)
            return None
        copies = []
        for s in list(range(1, nr)) + [0]:
            dest = lax.rem(mr + s, nr)
            part = back_part(k, dest)
            if s:
                store_packet(bsend.at[k, s], part)
                copies.append(send(bsend.at[k, s], brecv.at[k, s], bs.at[k, s], br.at[k, s], dest, mc))
            else:
                vox[k] = part
        return copies

    def back_sum(k, copies):
        if line:
            @pl.when(inner)
            def _():
                back_arrived(k, 3)
                vox[k] = vox[k] + load_packet(brecv.at[k, 3])

            total = vox[k]
            for slot in (2, 1):
                back_arrived(k, slot)
                total = total + load_packet(brecv.at[k, slot])
            return total
        total = vox[k]
        for i, copy in enumerate(copies):
            copy.wait_recv()
            total = total + load_packet(brecv.at[k, i + 1])
        return total

    def vox_take(k, origin):
        val = load_packet(vgat.at[k, origin])
        rows = pl.ds(pl.multiple_of(origin * sv, sv), sv)
        vfull[rows, :] = val
        xbf[rows, :] = val.astype(jnp.bfloat16)

    def grow(acc, mat, vec, first, depth, fresh):
        cols = pl.ds(pl.multiple_of(first, depth), depth)

        @pl.loop(0, acc.shape[0] // sv)
        def _(i):
            rows = pl.ds(pl.multiple_of(i * sv, sv), sv)
            val = dot(mat[rows, cols], vec[cols, :])
            acc[rows, :] = val if fresh else acc[rows, :] + val

    def vox_gather(k):
        store_packet(vgat.at[k, mr], vox[k])
        if line:
            def passed(origin, n, row):
                return row_copy(vgat.at[k, origin], vgat.at[k, origin], vs.at[k, n], vr.at[k, origin], row)

            @pl.when(inner)
            def _():
                passed(mr, 2, far).start()

            send(vgat.at[k, mr], vgat.at[k, mr], vs.at[k, 1], vr.at[k, mr], cross, mc)
            send(vgat.at[k, mr], vgat.at[k, mr], vs.at[k, 0], vr.at[k, mr], mate, mc)
            inner_sent.append(passed(mr, 2, far))
            inner_sent.append(passed(far, 3, mate))
            vox_take(k, mr)
            grow(facc, fa, xbf, mr * sv, sv, True)

            @pl.when(inner)
            def _():
                passed(far, 3, mate).wait_recv()
                passed(far, 3, mate).start()

            @pl.when(jnp.logical_not(inner))
            def _():
                passed(mate, 0, mate).wait_recv()

            vox_take(k, early)
            grow(facc, fa, xbf, early * sv, sv, False)
            passed(cross, 0, mate).wait_recv()
            vox_take(k, cross)
            grow(facc, fa, xbf, cross * sv, sv, False)
            passed(late, 0, mate).wait_recv()
            vox_take(k, late)
        else:
            copies = [
                send(vgat.at[k, mr], vgat.at[k, mr], vs.at[k, s], vr.at[k, s], lax.rem(mr + s, nr), mc)
                for s in range(1, nr)
            ]
            for copy in copies:
                copy.wait_recv()
            for q in range(nr):
                vox_take(k, q)
        return share(squares(vfull[...]), ncol.at[k], nc, mc, cs.at[k], cr.at[k], False)

    def fwd_part(first):
        rows = pl.ds(first, sr)
        if line:
            cols = pl.ds(pl.multiple_of(late * sv, sv), sv)
            return facc[rows, :] + dot(fa[rows, cols], xbf[cols, :])
        return dot(fa[rows, :], xbf[...])

    def fwd_start(k):
        order = list(range(1, nch)) + [0]
        local = []
        for s in order:
            q = lax.rem(chip + s, nch)
            first = pl.multiple_of((q * 2 + 1 - core) * sr, sr)
            dsend[k, s] = fwd_part(first)
            local.append(send(dsend.at[k, s], drecv.at[k, s], ds_.at[k, s], dr.at[k, s], mr, partner))
        copies = []
        for s, other in zip(order, local):
            q = lax.rem(chip + s, nch)
            first = pl.multiple_of((q * 2 + core) * sr, sr)
            part = fwd_part(first)
            other.wait_recv()
            part = part + drecv[k, s]
            if s:
                store_packet(fsend.at[k, s], part)
                copies.append(send(fsend.at[k, s], frecv.at[k, s], fs.at[k, s], fr.at[k, s], mr, q * 2 + core))
            else:
                ray[k + 1] = part
        return copies

    def fwd_sum(k, copies):
        total = ray[k + 1]
        for i, copy in enumerate(copies):
            copy.wait_recv()
            total = total + load_packet(frecv.at[k, i + 1])
        return total

    def ray_gather(k):
        store_packet(rgat.at[k, mc], ray[k + 1])
        across = [send(rgat.at[k, mc], rgat.at[k, mc], gs.at[k, 0], gr.at[k, 0], mr, partner)]
        for s in range(1, nch):
            peer = lax.rem(chip + s, nch) * 2 + core
            across.append(send(rgat.at[k, mc], rgat.at[k, mc], gs.at[k, s], gr.at[k, s], mr, peer))
        hand = [None]

        def take(origin):
            val = load_packet(rgat.at[k, origin])
            sq[origin] = jnp.broadcast_to(squares(val), (8, z))
            ybf[pl.ds(pl.multiple_of(origin * sr, sr), sr), :] = val.astype(jnp.bfloat16)

        take(mc)
        across[0].wait_recv()
        take(partner)
        grow(bacc, ba, ybf, chip * 2 * sr, 2 * sr, True)
        for s in range(1, nch):
            across[s].wait_recv()
            origin = lax.rem(chip + nch - s, nch) * 2 + core
            hand.append(send(rgat.at[k, origin], rgat.at[k, origin], hs.at[k, s], hr.at[k, s], mr, partner))
            take(origin)
        for s in range(1, nch):
            hand[s].wait_recv()
            origin = lax.rem(chip + nch - s, nch) * 2
            take(origin + 1 - core)
            if s + 1 < nch:
                grow(bacc, ba, ybf, origin * sr, 2 * sr, False)
        total = jnp.zeros((1, z), jnp.float32)
        for q in range(nc):
            total = total + sq[q][:1]
        return share(total, nrow.at[k + 1], nr, mr, rs.at[k + 1], rr.at[k + 1], True)

    ybf[...] = sino[...].astype(jnp.bfloat16)
    total = squares(sino[...])
    pl.semaphore_wait(barrier, nr - 1 + nc - 1)
    beta_of = share(total, nrow.at[0], nr, mr, rs.at[0], rr.at[0], True)
    copies = back_start(0)

    @pl.loop(0, tr)
    def _(i):
        first = pl.multiple_of(i * tile, tile)
        for j in range(tc):
            fa[pl.ds(first, tile), j * tile:(j + 1) * tile] = pick(i, j)

    beta = root(beta_of)
    ray[0] = sino[pl.ds(pl.multiple_of(mc * sr, sr), sr), :] * (1.0 / beta)
    vox[0] = back_sum(0, copies) * (1.0 / beta)
    alpha_of = vox_gather(0)
    phi_bar = beta
    for k in range(ITERS):
        copies = fwd_start(k)
        alpha = root(alpha_of)
        inv_alpha = 1.0 / alpha
        if k == 0:
            rho_bar = alpha
            sdir[...] = vfull[...] * inv_alpha
        else:
            theta = sine * alpha
            rho_bar = -cosine * alpha
            sdir[...] = vfull[...] * inv_alpha - (theta / rho) * sdir[...]
        vox[k] = vox[k] * inv_alpha
        ray_raw = fwd_sum(k, copies) * inv_alpha - alpha * ray[k]
        last = k + 1 == ITERS
        if last:
            total = share(squares(ray_raw), nlast, nc, mc, ls, lr, False)()
            beta = root(share(total, nrow.at[k + 1], nr, mr, rs.at[k + 1], rr.at[k + 1], True))
        else:
            ray[k + 1] = ray_raw
            beta_of = ray_gather(k)
            copies = back_start(k + 1)
            beta = root(beta_of)
            ray[k + 1] = ray[k + 1] * (1.0 / beta)
        rho = jnp.sqrt(rho_bar * rho_bar + beta * beta)
        cosine = rho_bar / rho
        sine = beta / rho
        phi = cosine * phi_bar
        phi_bar = sine * phi_bar
        step = (phi / rho) * sdir[...]
        sol[...] = step if k == 0 else sol[...] + step
        if not last:
            vox[k + 1] = back_sum(k + 1, copies) * (1.0 / beta) - beta * vox[k]
            alpha_of = vox_gather(k + 1)
    res[...] = jnp.broadcast_to(phi_bar, res.shape)
    for copy in sent:
        copy.wait_send()
    if line:
        @pl.when(inner)
        def _():
            for copy in inner_sent:
                copy.wait_send()


def body(nr, nc, tile_values, tile_rows, tile_cols, tile_count, sinogram):
    values = tile_values[0, 0]
    slots, tile = values.shape[0], values.shape[1]
    mb, z = sinogram.shape
    nb = TC * tile
    tr = mb // tile
    place = tile_rows[0, 0] * TC + tile_cols[0, 0]
    ids = jnp.arange(slots, dtype=jnp.int32)
    place = jnp.where(ids < tile_count[0, 0], place, -1)
    hit = place[None, :] == jnp.arange(tr * TC, dtype=jnp.int32)[:, None]
    inv = jnp.sum(jnp.where(hit, ids[None, :] + 1, 0), axis=1, dtype=jnp.int32) - 1
    nch = nc // 2
    sv, sr = nb // nr, mb // nc
    f32, bf16, i16 = jnp.float32, jnp.bfloat16, jnp.int16
    dma = pltpu.SemaphoreType.DMA
    vmem = pl.BlockSpec(memory_space=pltpu.VMEM)
    scratch = [
        pltpu.VMEM((mb, z), f32), pltpu.VMEM((nb, z), f32), pltpu.VMEM((nc, 8, z), f32),
        pltpu.VMEM((mb, nb), bf16), pltpu.VMEM((nb, mb), bf16),
        pltpu.VMEM((mb, z), bf16), pltpu.VMEM((nb, z), bf16),
        pltpu.VMEM((ITERS + 1, sr, z), f32), pltpu.VMEM((ITERS, sv, z), f32),
        pltpu.VMEM((nb, z), f32), pltpu.VMEM((nb, z), f32),
        pltpu.VMEM((ITERS, nr, sv + PAD, z), i16), pltpu.VMEM((ITERS, nr, sv + PAD, z), i16),
        pltpu.VMEM((ITERS, nr, sv + PAD, z), i16),
        pltpu.VMEM((ITERS, nch, sr, z), f32), pltpu.VMEM((ITERS, nch, sr, z), f32),
        pltpu.VMEM((ITERS, nch, sr + PAD, z), i16), pltpu.VMEM((ITERS, nch, sr + PAD, z), i16),
        pltpu.VMEM((ITERS, nc, sr + PAD, z), i16),
        pltpu.VMEM((ITERS + 1, nr, 8, z), f32), pltpu.VMEM((ITERS, nc, 8, z), f32),
        pltpu.VMEM((nc, 8, z), f32),
        dma((ITERS, nr)), dma((ITERS, nr)), dma((ITERS, nr)), dma((ITERS, nr)),
        dma((ITERS, nch)), dma((ITERS, nch)), dma((ITERS, nch)), dma((ITERS, nch)),
        dma((ITERS, nch)), dma((ITERS, nch)), dma((ITERS, nch)), dma((ITERS, nch)),
        dma((ITERS + 1, nr)), dma((ITERS + 1, nr)), dma((ITERS, nc)), dma((ITERS, nc)),
        dma((nc,)), dma((nc,)),
    ]
    sol, res = pl.pallas_call(
        functools.partial(kernel, nr, nc),
        out_shape=(jax.ShapeDtypeStruct((nb, z), f32), jax.ShapeDtypeStruct((8, z), f32)),
        in_specs=[pl.BlockSpec(memory_space=pltpu.SMEM), vmem, vmem],
        out_specs=(vmem, vmem),
        scratch_shapes=scratch,
        compiler_params=pltpu.CompilerParams(
            collective_id=0, has_side_effects=True, vmem_limit_bytes=60 * 1024 * 1024),
    )(inv, values, sinogram)
    return sol, res[0]


def solution(mesh):
    nr, nc = mesh.shape["row"], mesh.shape["col"]
    in_specs = (
        P("row", "col", None, None, None),
        P("row", "col", None),
        P("row", "col", None),
        P("row", "col"),
        P("row", None),
    )
    return jax.shard_map(
        functools.partial(body, nr, nc), mesh=mesh, in_specs=in_specs,
        out_specs=(P("col", None), P()), check_vma=False)
```

profile of v0, /device:TPU:0, one launch (start us, length us, event | category | flops | bytes accessed | tf_op | source)
XLA Modules:
  0.0 138.4 jit_solution(698074536255505265)
XLA Ops:
  1.3 0.7 compare_select_fusion
  2.0 0.1 select_reduce_fusion
  2.1 0.6 broadcast_add_fusion.inv
  2.6 132.3 %shard_map.68 = (f32[2048,128]{1,0:T(8,128)}, f32[8,128]{1,0:T(8,128)}) custom-call(s32[256]{0:T(256)} %broadcast_add_fusion.inv, bf16[128,128,128]{2,1,0:T(8,128)(2,1)} %bitcast.7, f32[2048,128]{1,0:T(8,128)} %sino.1), custom_call_target="tpu_custom_call" | custom-call | tf_op jit(solution)/shard_map/pallas_call | solution.py:417
  134.9 1.2 slice_bitcast_fusion
  136.1 2.3 %copy.9 = f32[2048,128]{1,0:T(8,128)} copy(f32[2048,128]{1,0:T(8,128)} %get-tuple-element.10) | data formatting | bytes 2097152
where the time goes:
time: 139 us; the launch traced here: 138 us
  Pallas kernels  132 us (95%)
  local copies, waits for them, and re-layouts  3.45 us (2%)
    pallas_call x1, Pallas kernels, body(): pl.pallas_call(functools.partial(kernel, nr, nc), out_shape=(jax.ShapeDty...  132 us

commit v1 on v0

--- a/solution.py
+++ b/solution.py
@@ -12,6 +12,8 @@
 EPSILON = 1e-06
 PAD = 16
 TOP = 32000.0
+FINE = 64.0
+LANE = 128
 MESH = pl.DeviceIdType.MESH
 
 
@@ -51,7 +53,7 @@
     return jnp.sum(vec * vec, axis=0, keepdims=True)
 
 
-def kernel(
+def kernel_rows(
     nr, nc, inv, tiles, sino, sol, res,
     facc, bacc, sq, fa, ba, ybf, xbf, ray, vox, vfull, sdir,
     bsend, brecv, vgat, dsend, drecv, fsend, frecv, rgat, nrow, ncol, nlast,
@@ -379,7 +381,7 @@
                 copy.wait_send()
 
 
-def body(nr, nc, tile_values, tile_rows, tile_cols, tile_count, sinogram):
+def body_rows(nr, nc, tile_values, tile_rows, tile_cols, tile_count, sinogram):
     values = tile_values[0, 0]
     slots, tile = values.shape[0], values.shape[1]
     mb, z = sinogram.shape
@@ -415,6 +417,462 @@
         dma((nc,)), dma((nc,)),
     ]
     sol, res = pl.pallas_call(
+        functools.partial(kernel_rows, nr, nc),
+        out_shape=(jax.ShapeDtypeStruct((nb, z), f32), jax.ShapeDtypeStruct((8, z), f32)),
+        in_specs=[pl.BlockSpec(memory_space=pltpu.SMEM), vmem, vmem],
+        out_specs=(vmem, vmem),
+        scratch_shapes=scratch,
+        compiler_params=pltpu.CompilerParams(
+            collective_id=0, has_side_effects=True, vmem_limit_bytes=60 * 1024 * 1024),
+    )(inv, values, sinogram)
+    return sol, res[0]
+
+
+def col_pack(ref, val):
+    h, n = val.shape
+    groups = h // PAD
+    mag = jnp.abs(val)
+    top = mag[:PAD]
+    for g in range(1, groups):
+        top = jnp.maximum(top, mag[g * PAD:(g + 1) * PAD])
+    top = jnp.max(top, axis=1, keepdims=True)
+    exponent = jnp.ceil(jnp.log2(jnp.maximum(top, 1e-30)) * FINE)
+    scale = jnp.concatenate([TOP * jnp.exp2(exponent * (-1.0 / FINE))] * groups, axis=0)
+    coded = jnp.round(val * scale).astype(jnp.int32).astype(jnp.int16)
+    for j in range(n // LANE):
+        ref[pl.ds(j * h, h), :] = coded[:, j * LANE:(j + 1) * LANE]
+    ref[pl.ds(n // LANE * h, PAD), :] = jnp.broadcast_to(exponent, (PAD, LANE)).astype(jnp.int32).astype(jnp.int16)
+
+
+def col_unpack(ref, h):
+    blocks = (ref.shape[0] - PAD) // h
+    exponent = ref[pl.ds(blocks * h, PAD), :].astype(jnp.int32).astype(jnp.float32)
+    scale = jnp.concatenate([jnp.exp2(exponent * (1.0 / FINE)) * (1.0 / TOP)] * (h // PAD), axis=0)
+    return jnp.concatenate(
+        [ref[pl.ds(j * h, h), :].astype(jnp.int32).astype(jnp.float32) * scale for j in range(blocks)], axis=1)
+
+
+def row_squares(val):
+    h, n = val.shape
+    acc = jnp.zeros((h, LANE), jnp.float32)
+    for j in range(n // LANE):
+        part = val[:, j * LANE:(j + 1) * LANE]
+        acc = acc + part * part
+    acc = jnp.concatenate([acc] * (LANE // h), axis=0)
+    return jnp.sum(acc.T, axis=0, keepdims=True)
+
+
+def kernel(
+    nr, nc, inv, tiles, sino, sol, res,
+    fa, ba, y0, yb, bacc, fpart, drecv, xb, vfull, ray, vox, relay, vrow, sdir,
+    bsend, brecv, vgat, fsend, frecv, zbuf, cbuf,
+    bs, br, vs, vr, ds_, dr, fs, fr, gs, gr, hs, hr, zs, zr, cs, cr,
+):
+    mr = lax.axis_index("row")
+    mc = lax.axis_index("col")
+    nch = nc // 2
+    chip = mc // 2
+    core = mc % 2
+    partner = chip * 2 + (1 - core)
+    tile = tiles.shape[1]
+    mb, z = sino.shape
+    nb = sol.shape[0]
+    tr, tc = mb // tile, nb // tile
+    sv, sr = nb // nr, mb // nc
+    hz = z // 2
+
+    inner = (mr == 1) | (mr == 2)
+    outer = jnp.logical_not(inner)
+    left = mr < 2
+    mate = mr + 1 - 2 * lax.rem(mr, 2)
+    cross = jnp.where(left, 2, 1)
+    far = jnp.where(left, 3, 0)
+    early = jnp.where(inner, far, mate)
+    late = jnp.where(inner, mate, far)
+
+    barrier = pltpu.get_barrier_semaphore()
+    for s in range(1, nr):
+        pl.semaphore_signal(barrier, 1, device_id=(lax.rem(mr + s, nr), mc), device_id_type=MESH)
+    for s in range(1, nc):
+        pl.semaphore_signal(barrier, 1, device_id=(mr, lax.rem(mc + s, nc)), device_id_type=MESH)
+
+    sent = []
+
+    def copy_to(src, dst, ssem, rsem, row, col):
+        return pltpu.make_async_remote_copy(
+            src_ref=src, dst_ref=dst, send_sem=ssem, recv_sem=rsem,
+            device_id=(row, col), device_id_type=MESH)
+
+    def send(src, dst, ssem, rsem, row, col):
+        copy = copy_to(src, dst, ssem, rsem, row, col)
+        copy.start()
+        sent.append(copy)
+        return copy
+
+    def block(first, size):
+        return pl.ds(pl.multiple_of(first, size), size)
+
+    def pick(i, j):
+        slot = inv[i * tc + j]
+        values = tiles[jnp.maximum(slot, 0)]
+        return jnp.where(slot >= 0, values, jnp.zeros_like(values))
+
+    def column(row, h):
+        return jnp.broadcast_to(row, (z, z)).T[h * hz:(h + 1) * hz]
+
+    def wide(col, n):
+        return jnp.concatenate([col] * (n // LANE), axis=1)
+
+    def merge(a, b):
+        lane = lax.broadcasted_iota(jnp.int32, (1, z), 1)
+        return jnp.where(lane < hz, a, b)
+
+    def share(vec, buf, n, me, ssem, rsem, over_row):
+        buf[me] = jnp.broadcast_to(vec, (8, z))
+        copies = []
+        for s in range(1, n):
+            peer = lax.rem(me + s, n)
+            place = (peer, mc) if over_row else (mr, peer)
+            copies.append(send(buf.at[me], buf.at[me], ssem.at[s], rsem.at[s], *place))
+
+        def finish():
+            for copy in copies:
+                copy.wait_recv()
+            total = buf[0]
+            for q in range(1, n):
+                total = total + buf[q]
+            return total[:1]
+
+        return finish
+
+    def share_z(vec, n, h):
+        return share(vec, zbuf.at[n, h], nr, mr, zs.at[n, h], zr.at[n, h], True)
+
+    def share_c(vec, n, h):
+        return share(vec, cbuf.at[n, h], nc, mc, cs.at[n, h], cr.at[n, h], False)
+
+    def back_part(k, h, dest):
+        cols = block(dest * sv, sv)
+        if k == 0:
+            if h == 0:
+                val = dot(y0[...], fa[:, cols])
+                bacc[1, dest] = val[hz:]
+                return val[:hz]
+            return bacc[1, dest]
+        val = bacc[h, dest]
+        q = lax.rem(chip + 1, nch) * 2
+        for i in range(2):
+            val = val + dot(yb[k, h, q + i], fa[block((q + i) * sr, sr), cols])
+        return val
+
+    def back_grow(k, h, q, fresh):
+        for d in range(nr):
+            cols = slice(d * sv, (d + 1) * sv)
+            val = dot(yb[k, h, q], fa[block(q * sr, sr), cols])
+            val = val + dot(yb[k, h, q + 1], fa[block((q + 1) * sr, sr), cols])
+            bacc[h, d] = val if fresh else bacc[h, d] + val
+
+    def back_start(k, h):
+        col_pack(bsend.at[k, h, 0], back_part(k, h, jnp.where(inner, cross, far)))
+        slot = jnp.where(inner, 3, 0)
+        send(bsend.at[k, h, 0], brecv.at[k, h, slot], bs.at[k, h, 0], br.at[k, h, slot],
+             jnp.where(inner, cross, mate), mc)
+        relay[h] = back_part(k, h, jnp.where(inner, far, cross))
+
+        @pl.when(outer)
+        def _():
+            col_pack(bsend.at[k, h, 1], relay[h])
+            copy_to(bsend.at[k, h, 1], brecv.at[k, h, 1], bs.at[k, h, 1], br.at[k, h, 1], cross, mc).start()
+
+        col_pack(bsend.at[k, h, 2], back_part(k, h, mate))
+        send(bsend.at[k, h, 2], brecv.at[k, h, 2], bs.at[k, h, 2], br.at[k, h, 2], mate, mc)
+        vox[k, h] = back_part(k, h, mr)
+
+    def back_arrived(k, h, slot):
+        copy_to(bsend.at[k, h, slot], brecv.at[k, h, slot], bs.at[k, h, slot], br.at[k, h, slot],
+                mate, mc).wait_recv()
+        return col_unpack(brecv.at[k, h, slot], hz)
+
+    def back_relay(k, h):
+        @pl.when(inner)
+        def _():
+            col_pack(bsend.at[k, h, 1], relay[h] + back_arrived(k, h, 0))
+            copy_to(bsend.at[k, h, 1], brecv.at[k, h, 1], bs.at[k, h, 1], br.at[k, h, 1], far, mc).start()
+
+        sent.append(copy_to(bsend.at[k, h, 1], brecv.at[k, h, 1], bs.at[k, h, 1], br.at[k, h, 1], mate, mc))
+
+    def back_sum(k, h):
+        @pl.when(inner)
+        def _():
+            vox[k, h] = vox[k, h] + back_arrived(k, h, 3)
+
+        total = vox[k, h] + back_arrived(k, h, 2)
+        return total + back_arrived(k, h, 1)
+
+    def fwd_grow(k, h, origin, fresh):
+        for q in range(nch):
+            cols = slice(2 * q * sr, 2 * (q + 1) * sr)
+            val = dot(xb[h, origin], ba[block(origin * sv, sv), cols])
+            for i in range(2):
+                half = val[:, i * sr:(i + 1) * sr]
+                fpart[k, h, 2 * q + i] = half if fresh else fpart[k, h, 2 * q + i] + half
+
+    def vox_take(k, h, origin):
+        val = col_unpack(vgat.at[k, h, origin], hz)
+        vfull[h, origin] = val
+        xb[h, origin] = val.astype(jnp.bfloat16)
+
+    def passed(k, h, origin, n, row):
+        own = vgat.at[k, h, origin]
+        return copy_to(own, own, vs.at[k, h, n], vr.at[k, h, origin], row, mc)
+
+    def vox_send(k, h):
+        @pl.when(inner)
+        def _():
+            passed(k, h, mr, 2, far).start()
+
+        own = vgat.at[k, h, mr]
+        send(own, own, vs.at[k, h, 1], vr.at[k, h, mr], cross, mc)
+        send(own, own, vs.at[k, h, 0], vr.at[k, h, mr], mate, mc)
+
+    def vox_early(k, h):
+        @pl.when(inner)
+        def _():
+            passed(k, h, far, 3, mate).wait_recv()
+            passed(k, h, far, 3, mate).start()
+
+        @pl.when(outer)
+        def _():
+            passed(k, h, mate, 0, mate).wait_recv()
+
+        vox_take(k, h, early)
+
+    def fwd_send(k, h):
+        local = []
+        for s in list(range(1, nch)) + [0]:
+            q = lax.rem(chip + s, nch) * 2
+            val = dot(xb[h, late], ba[block(late * sv, sv), block(q * sr, 2 * sr)])
+            for i in range(2):
+                fpart[k, h, q + i] = fpart[k, h, q + i] + val[:, i * sr:(i + 1) * sr]
+            local.append(send(fpart.at[k, h, q + 1 - core], drecv.at[k, h, s],
+                              ds_.at[k, h, s], dr.at[k, h, s], mr, partner))
+        return local
+
+    def fwd_pass(k, h, local):
+        copies = []
+        for s, other in zip(list(range(1, nch)) + [0], local):
+            q = lax.rem(chip + s, nch) * 2 + core
+            other.wait_recv()
+            part = fpart[k, h, q] + drecv[k, h, s]
+            if s:
+                col_pack(fsend.at[k, h, s], part)
+                copies.append(send(fsend.at[k, h, s], frecv.at[k, h, s], fs.at[k, h, s], fr.at[k, h, s], mr, q))
+            else:
+                ray[k + 1, h] = part
+        return copies
+
+    def fwd_sum(k, h, copies):
+        total = ray[k + 1, h]
+        for i, copy in enumerate(copies):
+            copy.wait_recv()
+            total = total + col_unpack(frecv.at[k, h, i + 1], hz)
+        return total
+
+    def flip(first, last):
+        @pl.loop(first, last)
+        def _(d):
+            for j in range(sv // LANE):
+                cols = slice(j * LANE, (j + 1) * LANE)
+                both = jnp.concatenate([vfull[0, d, :, cols], vfull[1, d, :, cols]], axis=0)
+                vrow[block(d * sv + j * LANE, LANE), :] = both.T
+
+    alphas = [[None, None] for _ in range(ITERS)]
+    betas = [[None, None] for _ in range(ITERS + 1)]
+    run = {}
+
+    def update_dir(k):
+        alpha = merge(*alphas[k])
+        inv_alpha = 1.0 / alpha
+        if k == 0:
+            run["rho_bar"] = alpha
+            sdir[...] = vrow[...] * inv_alpha
+        else:
+            theta = run["sine"] * alpha
+            run["rho_bar"] = -run["cosine"] * alpha
+            sdir[...] = vrow[...] * inv_alpha - (theta / run["rho"]) * sdir[...]
+
+    def update_sol(k):
+        beta = merge(*betas[k + 1])
+        rho_bar = run["rho_bar"]
+        rho = jnp.sqrt(rho_bar * rho_bar + beta * beta)
+        run["rho"] = rho
+        run["cosine"] = rho_bar / rho
+        run["sine"] = beta / rho
+        phi = run["cosine"] * run["phi_bar"]
+        run["phi_bar"] = run["sine"] * run["phi_bar"]
+        step = (phi / rho) * sdir[...]
+        sol[...] = step if k == 0 else sol[...] + step
+
+    def half(h):
+        beta_of = None
+        for k in range(ITERS):
+            back_start(k, h)
+            yield
+            back_relay(k, h)
+            yield
+            total = back_sum(k, h)
+            if k:
+                betas[k][h] = root(beta_of)
+            beta = betas[k][h]
+            raw = total * wide(column(1.0 / beta, h), sv)
+            if k:
+                raw = raw - wide(column(beta / alphas[k - 1][h], h), sv) * vox[k - 1, h]
+            vox[k, h] = raw
+            col_pack(vgat.at[k, h, mr], raw)
+            vox_send(k, h)
+            alpha_of = share_z(row_squares(raw), 2 * k + 1, h)
+            vox_take(k, h, mr)
+            if k == 0 and h == 0:
+                build_ba()
+            fwd_grow(k, h, mr, True)
+            if k and h:
+                update_sol(k - 1)
+            yield
+            vox_early(k, h)
+            fwd_grow(k, h, early, False)
+            yield
+            passed(k, h, cross, 0, mate).wait_recv()
+            vox_take(k, h, cross)
+            fwd_grow(k, h, cross, False)
+            yield
+            passed(k, h, late, 0, mate).wait_recv()
+            vox_take(k, h, late)
+            local = fwd_send(k, h)
+            alpha_of = share_c(alpha_of(), 2 * k + 1, h)
+            yield
+            copies = fwd_pass(k, h, local)
+            if h:
+                flip(0, nr)
+            yield
+            total = fwd_sum(k, h, copies)
+            alpha = root(alpha_of)
+            alphas[k][h] = alpha
+            raw = total * wide(column(1.0 / alpha, h), sr)
+            raw = raw - wide(column(alpha / beta, h), sr) * ray[k, h]
+            n = 2 * k + 2
+            if k + 1 == ITERS:
+                beta_of = share_c(row_squares(raw), n, h)
+                if h:
+                    update_dir(k)
+                yield
+                beta_of = share_z(beta_of(), n, h)
+                yield
+                betas[k + 1][h] = root(beta_of)
+                return
+            ray[k + 1, h] = raw
+            own = yb.at[k + 1, h, mc]
+            own[...] = raw.astype(jnp.bfloat16)
+            across = [send(own, own, gs.at[k, h, 0], gr.at[k, h, 0], mr, partner)]
+            for s in range(1, nch):
+                peer = lax.rem(chip + s, nch) * 2 + core
+                across.append(send(own, own, gs.at[k, h, s], gr.at[k, h, s], mr, peer))
+            beta_of = share_c(row_squares(raw), n, h)
+            if h:
+                update_dir(k)
+            yield
+            across[0].wait_recv()
+            back_grow(k + 1, h, chip * 2, True)
+            yield
+            hand = [None]
+            for s in range(1, nch):
+                across[s].wait_recv()
+                origin = lax.rem(chip + nch - s, nch) * 2 + core
+                given = yb.at[k + 1, h, origin]
+                hand.append(send(given, given, hs.at[k, h, s], hr.at[k, h, s], mr, partner))
+            beta_of = share_z(beta_of(), n, h)
+            yield
+            for s in range(1, nch):
+                hand[s].wait_recv()
+                if s + 1 < nch:
+                    back_grow(k + 1, h, lax.rem(chip + nch - s, nch) * 2, False)
+
+    def build_ba():
+        @pl.loop(0, tc)
+        def _(j):
+            for i in range(tr):
+                ba[block(j * tile, tile), i * tile:(i + 1) * tile] = pick(i, j).T
+
+    @pl.loop(0, tr)
+    def _(i):
+        for j in range(tc):
+            fa[block(i * tile, tile), j * tile:(j + 1) * tile] = pick(i, j)
+
+    total = squares(sino[...])
+    pl.semaphore_wait(barrier, nr - 1 + nc - 1)
+    beta_of = share_z(total, 0, 0)
+    for i in range(tr):
+        y0[:, i * tile:(i + 1) * tile] = sino[i * tile:(i + 1) * tile, :].T.astype(jnp.bfloat16)
+    own = sino[block(mc * sr, sr), :].T
+    ray[0, 0] = own[:hz]
+    ray[0, 1] = own[hz:]
+    beta = root(beta_of)
+    betas[0] = [beta, beta]
+    run["phi_bar"] = beta
+    live = [half(0), half(1)]
+    while live:
+        for one in list(live):
+            try:
+                next(one)
+            except StopIteration:
+                live.remove(one)
+    update_sol(ITERS - 1)
+    res[...] = jnp.broadcast_to(run["phi_bar"], res.shape)
+    for copy in sent:
+        copy.wait_send()
+
+    @pl.when(inner)
+    def _():
+        for k in range(ITERS):
+            for h in range(2):
+                passed(k, h, mr, 2, far).wait_send()
+                passed(k, h, far, 3, mate).wait_send()
+
+
+def body(nr, nc, tile_values, tile_rows, tile_cols, tile_count, sinogram):
+    values = tile_values[0, 0]
+    slots, tile = values.shape[0], values.shape[1]
+    mb, z = sinogram.shape
+    nb = TC * tile
+    tr = mb // tile
+    sv, sr = nb // nr, mb // nc
+    if nr != 4 or nc % 2 or sr % LANE or sv % LANE or z != LANE:
+        return body_rows(nr, nc, tile_values, tile_rows, tile_cols, tile_count, sinogram)
+    place = tile_rows[0, 0] * TC + tile_cols[0, 0]
+    ids = jnp.arange(slots, dtype=jnp.int32)
+    place = jnp.where(ids < tile_count[0, 0], place, -1)
+    hit = place[None, :] == jnp.arange(tr * TC, dtype=jnp.int32)[:, None]
+    inv = jnp.sum(jnp.where(hit, ids[None, :] + 1, 0), axis=1, dtype=jnp.int32) - 1
+    nch, hz = nc // 2, z // 2
+    f32, bf16, i16 = jnp.float32, jnp.bfloat16, jnp.int16
+    dma, vmem_of = pltpu.SemaphoreType.DMA, pltpu.VMEM
+    vmem = pl.BlockSpec(memory_space=pltpu.VMEM)
+    pb, pf = sv // LANE * hz + PAD, sr // LANE * hz + PAD
+    norms = 2 * ITERS + 1
+    scratch = [
+        vmem_of((mb, nb), bf16), vmem_of((nb, mb), bf16), vmem_of((z, mb), bf16),
+        vmem_of((ITERS, 2, nc, hz, sr), bf16), vmem_of((2, nr, hz, sv), f32),
+        vmem_of((ITERS, 2, nc, hz, sr), f32), vmem_of((ITERS, 2, nch, hz, sr), f32),
+        vmem_of((2, nr, hz, sv), bf16), vmem_of((2, nr, hz, sv), f32),
+        vmem_of((ITERS + 1, 2, hz, sr), f32), vmem_of((ITERS, 2, hz, sv), f32), vmem_of((2, hz, sv), f32),
+        vmem_of((nb, z), f32), vmem_of((nb, z), f32),
+        vmem_of((ITERS, 2, nr, pb, LANE), i16), vmem_of((ITERS, 2, nr, pb, LANE), i16),
+        vmem_of((ITERS, 2, nr, pb, LANE), i16),
+        vmem_of((ITERS, 2, nch, pf, LANE), i16), vmem_of((ITERS, 2, nch, pf, LANE), i16),
+        vmem_of((norms, 2, nr, 8, z), f32), vmem_of((norms, 2, nc, 8, z), f32),
+    ] + [dma((ITERS, 2, nr))] * 4 + [dma((ITERS, 2, nch))] * 8 + [
+        dma((norms, 2, nr)), dma((norms, 2, nr)), dma((norms, 2, nc)), dma((norms, 2, nc)),
+    ]
+    sol, res = pl.pallas_call(
         functools.partial(kernel, nr, nc),
         out_shape=(jax.ShapeDtypeStruct((nb, z), f32), jax.ShapeDtypeStruct((8, z), f32)),
         in_specs=[pl.BlockSpec(memory_space=pltpu.SMEM), vmem, vmem],

time: 139 us -> 131 us (0.942)
  Pallas kernels: 132 us -> 124 us
    pallas_call x1, Pallas kernels: 132 us -> 124 us  [body(): pl.pallas_call(functools.partial(kernel, nr, nc), out_shape=(jax.ShapeDty...]
where the time goes in v1:
time: 131 us
  Pallas kernels  124 us (95%)
  local copies, waits for them, and re-layouts  3.45 us (3%)
  other arithmetic  1.36 us (1%)
    pallas_call x1, Pallas kernels, body(): pl.pallas_call(functools.partial(kernel, nr, nc), out_shape=(jax.ShapeDty...  124 us

profile of v1, /device:TPU:0, one launch (start us, length us, event | category | flops | bytes accessed | tf_op | source)
XLA Modules:
  0.0 130.6 jit_solution(12736384652915694087)
XLA Ops:
  1.3 0.7 compare_select_fusion
  2.0 0.1 select_reduce_fusion
  2.1 0.6 broadcast_add_fusion.inv
  2.6 124.5 %shard_map.68 = (f32[2048,128]{1,0:T(8,128)}, f32[8,128]{1,0:T(8,128)}) custom-call(s32[256]{0:T(256)} %broadcast_add_fusion.inv, bf16[128,128,128]{2,1,0:T(8,128)(2,1)} %bitcast.7, f32[2048,128]{1,0:T(8,128)} %sino.1), custom_call_target="tpu_custom_call" | custom-call | tf_op jit(solution)/shard_map/pallas_call | solution.py:875
  127.1 1.2 slice_bitcast_fusion
  128.3 2.3 %copy.9 = f32[2048,128]{1,0:T(8,128)} copy(f32[2048,128]{1,0:T(8,128)} %get-tuple-element.10) | data formatting | bytes 2097152

commit v2 on v1

--- a/solution.py
+++ b/solution.py
@@ -14,6 +14,8 @@
 TOP = 32000.0
 FINE = 64.0
 LANE = 128
+GRANT = 53000 * 1024
+ORDER = [0, 1] * 10 * ITERS
 MESH = pl.DeviceIdType.MESH
 
 
@@ -463,10 +465,11 @@
 
 
 def kernel(
-    nr, nc, inv, tiles, sino, sol, res,
-    fa, ba, y0, yb, bacc, fpart, drecv, xb, vfull, ray, vox, relay, vrow, sdir,
+    nr, nc, place_of, tiles_in, sino_in, sol, sdir, res,
+    tiles, sino, inv_row, inv,
+    fa, ba, y0, yb, bacc, fpart, drecv, xb, vfull, ray, vox, relay, vrow,
     bsend, brecv, vgat, fsend, frecv, zbuf, cbuf,
-    bs, br, vs, vr, ds_, dr, fs, fr, gs, gr, hs, hr, zs, zr, cs, cr,
+    bs, br, vs, vr, ds_, dr, fs, fr, gs, gr, hs, hr, zs, zr, cs, cr, io,
 ):
     mr = lax.axis_index("row")
     mc = lax.axis_index("col")
@@ -474,7 +477,7 @@
     chip = mc // 2
     core = mc % 2
     partner = chip * 2 + (1 - core)
-    tile = tiles.shape[1]
+    slots, tile = tiles_in.shape[0], tiles_in.shape[1]
     mb, z = sino.shape
     nb = sol.shape[0]
     tr, tc = mb // tile, nb // tile
@@ -495,27 +498,42 @@
         pl.semaphore_signal(barrier, 1, device_id=(lax.rem(mr + s, nr), mc), device_id_type=MESH)
     for s in range(1, nc):
         pl.semaphore_signal(barrier, 1, device_id=(mr, lax.rem(mc + s, nc)), device_id_type=MESH)
-
-    sent = []
+    load_sino = pltpu.make_async_copy(sino_in, sino, io.at[0])
+    load_sino.start()
+    load_tiles = []
+    for i in range(4):
+        some = pl.ds(slots // 4 * i, slots // 4)
+        load_tiles.append(pltpu.make_async_copy(tiles_in.at[some], tiles.at[some], io.at[i + 2]))
+        load_tiles[i].start()
+
+    pending = {}
 
     def copy_to(src, dst, ssem, rsem, row, col):
         return pltpu.make_async_remote_copy(
             src_ref=src, dst_ref=dst, send_sem=ssem, recv_sem=rsem,
             device_id=(row, col), device_id_type=MESH)
 
-    def send(src, dst, ssem, rsem, row, col):
-        copy = copy_to(src, dst, ssem, rsem, row, col)
+    def settle(key):
+        if key in pending:
+            pending.pop(key).wait_send()
+
+    def send(src, dst, ssems, rsems, h, s, slot, row, col):
+        key = (id(ssems), h, s)
+        settle(key)
+        copy = copy_to(src, dst, ssems.at[h, s], rsems.at[h, slot], row, col)
         copy.start()
-        sent.append(copy)
+        pending[key] = copy
         return copy
+
+    def chip_at(s):
+        return (chip // 2 + s // 2) % 2 * 2 + (chip % 2 + s % 2) % 2
 
     def block(first, size):
         return pl.ds(pl.multiple_of(first, size), size)
 
     def pick(i, j):
-        slot = inv[i * tc + j]
-        values = tiles[jnp.maximum(slot, 0)]
-        return jnp.where(slot >= 0, values, jnp.zeros_like(values))
+        per = LANE // tc
+        return tiles[inv[i // per, i % per * tc + j]]
 
     def column(row, h):
         return jnp.broadcast_to(row, (z, z)).T[h * hz:(h + 1) * hz]
@@ -527,17 +545,20 @@
         lane = lax.broadcasted_iota(jnp.int32, (1, z), 1)
         return jnp.where(lane < hz, a, b)
 
-    def share(vec, buf, n, me, ssem, rsem, over_row):
+    def share(vec, buf, n, me, ssems, rsems, kind, h, over_row):
+        key = (id(ssems), kind, h)
+        settle(key)
         buf[me] = jnp.broadcast_to(vec, (8, z))
-        copies = []
         for s in range(1, n):
             peer = lax.rem(me + s, n)
             place = (peer, mc) if over_row else (mr, peer)
-            copies.append(send(buf.at[me], buf.at[me], ssem.at[s], rsem.at[s], *place))
+            copy_to(buf.at[me], buf.at[me], ssems.at[kind, h], rsems.at[kind, h], *place).start()
+        others = buf.at[pl.ds(0, n - 1)]
+        place = (lax.rem(mr + 1, nr), mc)
+        pending[key] = copy_to(others, others, ssems.at[kind, h], rsems.at[kind, h], *place)
 
         def finish():
-            for copy in copies:
-                copy.wait_recv()
+            copy_to(others, others, ssems.at[kind, h], rsems.at[kind, h], *place).wait_recv()
             total = buf[0]
             for q in range(1, n):
                 total = total + buf[q]
@@ -546,21 +567,22 @@
         return finish
 
     def share_z(vec, n, h):
-        return share(vec, zbuf.at[n, h], nr, mr, zs.at[n, h], zr.at[n, h], True)
+        return share(vec, zbuf.at[n, h], nr, mr, zs, zr, n % 2, h, True)
 
     def share_c(vec, n, h):
-        return share(vec, cbuf.at[n, h], nc, mc, cs.at[n, h], cr.at[n, h], False)
+        return share(vec, cbuf.at[n, h], nc, mc, cs, cr, n % 2, h, False)
 
     def back_part(k, h, dest):
         cols = block(dest * sv, sv)
         if k == 0:
             if h == 0:
+                build_fa(dest)
                 val = dot(y0[...], fa[:, cols])
                 bacc[1, dest] = val[hz:]
                 return val[:hz]
             return bacc[1, dest]
         val = bacc[h, dest]
-        q = lax.rem(chip + 1, nch) * 2
+        q = chip_at(1) * 2
         for i in range(2):
             val = val + dot(yb[k, h, q + i], fa[block((q + i) * sr, sr), cols])
         return val
@@ -575,31 +597,30 @@
     def back_start(k, h):
         col_pack(bsend.at[k, h, 0], back_part(k, h, jnp.where(inner, cross, far)))
         slot = jnp.where(inner, 3, 0)
-        send(bsend.at[k, h, 0], brecv.at[k, h, slot], bs.at[k, h, 0], br.at[k, h, slot],
-             jnp.where(inner, cross, mate), mc)
+        send(bsend.at[k, h, 0], brecv.at[k, h, slot], bs, br, h, 0, slot, jnp.where(inner, cross, mate), mc)
+        settle((id(bs), h, 1))
         relay[h] = back_part(k, h, jnp.where(inner, far, cross))
 
         @pl.when(outer)
         def _():
             col_pack(bsend.at[k, h, 1], relay[h])
-            copy_to(bsend.at[k, h, 1], brecv.at[k, h, 1], bs.at[k, h, 1], br.at[k, h, 1], cross, mc).start()
+            copy_to(bsend.at[k, h, 1], brecv.at[k, h, 1], bs.at[h, 1], br.at[h, 1], cross, mc).start()
 
         col_pack(bsend.at[k, h, 2], back_part(k, h, mate))
-        send(bsend.at[k, h, 2], brecv.at[k, h, 2], bs.at[k, h, 2], br.at[k, h, 2], mate, mc)
+        send(bsend.at[k, h, 2], brecv.at[k, h, 2], bs, br, h, 2, 2, mate, mc)
         vox[k, h] = back_part(k, h, mr)
 
     def back_arrived(k, h, slot):
-        copy_to(bsend.at[k, h, slot], brecv.at[k, h, slot], bs.at[k, h, slot], br.at[k, h, slot],
-                mate, mc).wait_recv()
+        copy_to(bsend.at[k, h, slot], brecv.at[k, h, slot], bs.at[h, slot], br.at[h, slot], mate, mc).wait_recv()
         return col_unpack(brecv.at[k, h, slot], hz)
 
     def back_relay(k, h):
         @pl.when(inner)
         def _():
             col_pack(bsend.at[k, h, 1], relay[h] + back_arrived(k, h, 0))
-            copy_to(bsend.at[k, h, 1], brecv.at[k, h, 1], bs.at[k, h, 1], br.at[k, h, 1], far, mc).start()
-
-        sent.append(copy_to(bsend.at[k, h, 1], brecv.at[k, h, 1], bs.at[k, h, 1], br.at[k, h, 1], mate, mc))
+            copy_to(bsend.at[k, h, 1], brecv.at[k, h, 1], bs.at[h, 1], br.at[h, 1], far, mc).start()
+
+        pending[id(bs), h, 1] = copy_to(bsend.at[k, h, 1], brecv.at[k, h, 1], bs.at[h, 1], br.at[h, 1], mate, mc)
 
     def back_sum(k, h):
         @pl.when(inner)
@@ -624,16 +645,19 @@
 
     def passed(k, h, origin, n, row):
         own = vgat.at[k, h, origin]
-        return copy_to(own, own, vs.at[k, h, n], vr.at[k, h, origin], row, mc)
+        return copy_to(own, own, vs.at[h, n], vr.at[h, origin], row, mc)
 
     def vox_send(k, h):
         @pl.when(inner)
         def _():
+            if k:
+                passed(k, h, mr, 2, far).wait_send()
+                passed(k, h, far, 3, mate).wait_send()
             passed(k, h, mr, 2, far).start()
 
         own = vgat.at[k, h, mr]
-        send(own, own, vs.at[k, h, 1], vr.at[k, h, mr], cross, mc)
-        send(own, own, vs.at[k, h, 0], vr.at[k, h, mr], mate, mc)
+        send(own, own, vs, vr, h, 1, mr, cross, mc)
+        send(own, own, vs, vr, h, 0, mr, mate, mc)
 
     def vox_early(k, h):
         @pl.when(inner)
@@ -649,24 +673,23 @@
 
     def fwd_send(k, h):
         local = []
-        for s in list(range(1, nch)) + [0]:
-            q = lax.rem(chip + s, nch) * 2
+        for s in range(nch - 1, -1, -1):
+            q = chip_at(s) * 2
             val = dot(xb[h, late], ba[block(late * sv, sv), block(q * sr, 2 * sr)])
             for i in range(2):
                 fpart[k, h, q + i] = fpart[k, h, q + i] + val[:, i * sr:(i + 1) * sr]
-            local.append(send(fpart.at[k, h, q + 1 - core], drecv.at[k, h, s],
-                              ds_.at[k, h, s], dr.at[k, h, s], mr, partner))
+            local.append(send(fpart.at[k, h, q + 1 - core], drecv.at[k, h, s], ds_, dr, h, s, s, mr, partner))
         return local
 
     def fwd_pass(k, h, local):
         copies = []
-        for s, other in zip(list(range(1, nch)) + [0], local):
-            q = lax.rem(chip + s, nch) * 2 + core
+        for s, other in zip(range(nch - 1, -1, -1), local):
+            q = chip_at(s) * 2 + core
             other.wait_recv()
             part = fpart[k, h, q] + drecv[k, h, s]
             if s:
                 col_pack(fsend.at[k, h, s], part)
-                copies.append(send(fsend.at[k, h, s], frecv.at[k, h, s], fs.at[k, h, s], fr.at[k, h, s], mr, q))
+                copies.append(send(fsend.at[k, h, s], frecv.at[k, h, s], fs, fr, h, s, s, mr, q))
             else:
                 ray[k + 1, h] = part
         return copies
@@ -675,7 +698,7 @@
         total = ray[k + 1, h]
         for i, copy in enumerate(copies):
             copy.wait_recv()
-            total = total + col_unpack(frecv.at[k, h, i + 1], hz)
+            total = total + col_unpack(frecv.at[k, h, nch - 1 - i], hz)
         return total
 
     def flip(first, last):
@@ -710,6 +733,10 @@
         run["sine"] = beta / rho
         phi = run["cosine"] * run["phi_bar"]
         run["phi_bar"] = run["sine"] * run["phi_bar"]
+        if k + 1 == ITERS:
+            res[0:8] = jnp.broadcast_to(phi / rho, (8, z))
+            res[8:16] = jnp.broadcast_to(run["phi_bar"], (8, z))
+            return
         step = (phi / rho) * sdir[...]
         sol[...] = step if k == 0 else sol[...] + step
 
@@ -717,12 +744,21 @@
         beta_of = None
         for k in range(ITERS):
             back_start(k, h)
+            if k == 0 and h:
+                build_ba(mr)
             yield
             back_relay(k, h)
+            if k == 0:
+                build_ba(cross if h else early)
             yield
+            if k == 0 and h:
+                build_ba(late)
             total = back_sum(k, h)
             if k:
                 betas[k][h] = root(beta_of)
+            elif not h:
+                run["phi_bar"] = root(first_norm)
+                betas[0] = [run["phi_bar"], run["phi_bar"]]
             beta = betas[k][h]
             raw = total * wide(column(1.0 / beta, h), sv)
             if k:
@@ -732,8 +768,6 @@
             vox_send(k, h)
             alpha_of = share_z(row_squares(raw), 2 * k + 1, h)
             vox_take(k, h, mr)
-            if k == 0 and h == 0:
-                build_ba()
             fwd_grow(k, h, mr, True)
             if k and h:
                 update_sol(k - 1)
@@ -772,10 +806,9 @@
             ray[k + 1, h] = raw
             own = yb.at[k + 1, h, mc]
             own[...] = raw.astype(jnp.bfloat16)
-            across = [send(own, own, gs.at[k, h, 0], gr.at[k, h, 0], mr, partner)]
-            for s in range(1, nch):
-                peer = lax.rem(chip + s, nch) * 2 + core
-                across.append(send(own, own, gs.at[k, h, s], gr.at[k, h, s], mr, peer))
+            across = [send(own, own, gs, gr, h, 0, 0, mr, partner)]
+            for s in range(nch - 1, 0, -1):
+                across.append(send(own, own, gs, gr, h, s, s, mr, chip_at(s) * 2 + core))
             beta_of = share_c(row_squares(raw), n, h)
             if h:
                 update_dir(k)
@@ -783,59 +816,82 @@
             across[0].wait_recv()
             back_grow(k + 1, h, chip * 2, True)
             yield
-            hand = [None]
-            for s in range(1, nch):
-                across[s].wait_recv()
-                origin = lax.rem(chip + nch - s, nch) * 2 + core
+            hand = []
+            for s in range(nch - 1, 0, -1):
+                across[nch - s].wait_recv()
+                origin = chip_at(s) * 2 + core
                 given = yb.at[k + 1, h, origin]
-                hand.append(send(given, given, hs.at[k, h, s], hr.at[k, h, s], mr, partner))
+                hand.append(send(given, given, hs, hr, h, s, s, mr, partner))
             beta_of = share_z(beta_of(), n, h)
             yield
-            for s in range(1, nch):
-                hand[s].wait_recv()
-                if s + 1 < nch:
-                    back_grow(k + 1, h, lax.rem(chip + nch - s, nch) * 2, False)
-
-    def build_ba():
-        @pl.loop(0, tc)
+            for s in range(nch - 1, 0, -1):
+                hand[nch - 1 - s].wait_recv()
+                if s > 1:
+                    back_grow(k + 1, h, chip_at(s) * 2, False)
+
+    def build_fa(dest):
+        wide_by = sv // tile
+
+        @pl.loop(0, tr)
+        def _(i):
+            for j in range(wide_by):
+                fa[block(i * tile, tile), block(dest * sv + j * tile, tile)] = pick(i, dest * wide_by + j)
+
+    def build_ba(origin):
+        wide_by = sv // tile
+
+        @pl.loop(0, wide_by)
         def _(j):
             for i in range(tr):
-                ba[block(j * tile, tile), i * tile:(i + 1) * tile] = pick(i, j).T
-
-    @pl.loop(0, tr)
-    def _(i):
-        for j in range(tc):
-            fa[block(i * tile, tile), j * tile:(j + 1) * tile] = pick(i, j)
-
+                ba[block(origin * sv + j * tile, tile), i * tile:(i + 1) * tile] = pick(i, origin * wide_by + j).T
+
+    place = jnp.broadcast_to(place_of[...], (LANE, slots)).T
+    slot_of = lax.broadcasted_iota(jnp.int32, (slots, LANE), 0)
+    for i in range(inv.shape[0]):
+        spot = lax.broadcasted_iota(jnp.int32, (slots, LANE), 1) + i * LANE
+        inv_row[i:i + 1, :] = jnp.min(jnp.where(place == spot, slot_of, slots), axis=0, keepdims=True)
+    move = pltpu.make_async_copy(inv_row, inv, io.at[1])
+    move.start()
+    tiles[slots] = jnp.zeros((tile, tile), tiles.dtype)
+    load_sino.wait()
     total = squares(sino[...])
-    pl.semaphore_wait(barrier, nr - 1 + nc - 1)
-    beta_of = share_z(total, 0, 0)
     for i in range(tr):
         y0[:, i * tile:(i + 1) * tile] = sino[i * tile:(i + 1) * tile, :].T.astype(jnp.bfloat16)
     own = sino[block(mc * sr, sr), :].T
     ray[0, 0] = own[:hz]
     ray[0, 1] = own[hz:]
-    beta = root(beta_of)
-    betas[0] = [beta, beta]
-    run["phi_bar"] = beta
-    live = [half(0), half(1)]
-    while live:
-        for one in list(live):
-            try:
-                next(one)
-            except StopIteration:
-                live.remove(one)
+    move.wait()
+    for load in load_tiles:
+        load.wait()
+
+    pl.semaphore_wait(barrier, nr - 1 + nc - 1)
+    first_norm = share_z(total, 0, 0)
+    halves = [half(0), half(1)]
+    for h in ORDER:
+        next(halves[h], None)
     update_sol(ITERS - 1)
-    res[...] = jnp.broadcast_to(run["phi_bar"], res.shape)
-    for copy in sent:
-        copy.wait_send()
+    for key in list(pending):
+        settle(key)
 
     @pl.when(inner)
     def _():
-        for k in range(ITERS):
-            for h in range(2):
-                passed(k, h, mr, 2, far).wait_send()
-                passed(k, h, far, 3, mate).wait_send()
+        for h in range(2):
+            passed(0, h, mr, 2, far).wait_send()
+            passed(0, h, far, 3, mate).wait_send()
+
+
+def finish_kernel(x, d, scale, out, last, val, sems):
+    parts = sems.shape[0]
+    n = x.shape[0] // parts
+    last[...] = scale[8:9, :]
+    stores = []
+    for i in range(parts):
+        rows = pl.ds(i * n, n)
+        val[rows, :] = x[rows, :] + scale[0:1, :] * d[rows, :]
+        stores.append(pltpu.make_async_copy(val.at[rows], out.at[rows], sems.at[i]))
+        stores[i].start()
+    for store in stores:
+        store.wait()
 
 
 def body(nr, nc, tile_values, tile_rows, tile_cols, tile_count, sinogram):
@@ -845,43 +901,51 @@
     nb = TC * tile
     tr = mb // tile
     sv, sr = nb // nr, mb // nc
-    if nr != 4 or nc % 2 or sr % LANE or sv % LANE or z != LANE:
+    if nr != 4 or nc != 8 or sr % LANE or sv % LANE or z != LANE:
         return body_rows(nr, nc, tile_values, tile_rows, tile_cols, tile_count, sinogram)
-    place = tile_rows[0, 0] * TC + tile_cols[0, 0]
-    ids = jnp.arange(slots, dtype=jnp.int32)
-    place = jnp.where(ids < tile_count[0, 0], place, -1)
-    hit = place[None, :] == jnp.arange(tr * TC, dtype=jnp.int32)[:, None]
-    inv = jnp.sum(jnp.where(hit, ids[None, :] + 1, 0), axis=1, dtype=jnp.int32) - 1
+    ids = jnp.arange(slots, dtype=jnp.int32)[None, :]
+    place = jnp.where(ids < tile_count, tile_rows[0] * TC + tile_cols[0], -1)
     nch, hz = nc // 2, z // 2
     f32, bf16, i16 = jnp.float32, jnp.bfloat16, jnp.int16
     dma, vmem_of = pltpu.SemaphoreType.DMA, pltpu.VMEM
     vmem = pl.BlockSpec(memory_space=pltpu.VMEM)
+    hbm = pl.BlockSpec(memory_space=pltpu.HBM)
     pb, pf = sv // LANE * hz + PAD, sr // LANE * hz + PAD
     norms = 2 * ITERS + 1
+    spots = tr * TC // LANE
     scratch = [
+        vmem_of((slots + 1, tile, tile), bf16), vmem_of((mb, z), f32),
+        vmem_of((spots, LANE), jnp.int32), pltpu.SMEM((spots, LANE), jnp.int32),
         vmem_of((mb, nb), bf16), vmem_of((nb, mb), bf16), vmem_of((z, mb), bf16),
         vmem_of((ITERS, 2, nc, hz, sr), bf16), vmem_of((2, nr, hz, sv), f32),
         vmem_of((ITERS, 2, nc, hz, sr), f32), vmem_of((ITERS, 2, nch, hz, sr), f32),
         vmem_of((2, nr, hz, sv), bf16), vmem_of((2, nr, hz, sv), f32),
         vmem_of((ITERS + 1, 2, hz, sr), f32), vmem_of((ITERS, 2, hz, sv), f32), vmem_of((2, hz, sv), f32),
-        vmem_of((nb, z), f32), vmem_of((nb, z), f32),
+        vmem_of((nb, z), f32),
         vmem_of((ITERS, 2, nr, pb, LANE), i16), vmem_of((ITERS, 2, nr, pb, LANE), i16),
         vmem_of((ITERS, 2, nr, pb, LANE), i16),
         vmem_of((ITERS, 2, nch, pf, LANE), i16), vmem_of((ITERS, 2, nch, pf, LANE), i16),
         vmem_of((norms, 2, nr, 8, z), f32), vmem_of((norms, 2, nc, 8, z), f32),
-    ] + [dma((ITERS, 2, nr))] * 4 + [dma((ITERS, 2, nch))] * 8 + [
-        dma((norms, 2, nr)), dma((norms, 2, nr)), dma((norms, 2, nc)), dma((norms, 2, nc)),
-    ]
-    sol, res = pl.pallas_call(
+    ] + [dma((2, nr))] * 4 + [dma((2, nch))] * 8 + [dma((2, 2))] * 4 + [dma((6,))]
+    part = jax.ShapeDtypeStruct((nb, z), f32)
+    sol, step, scale = pl.pallas_call(
         functools.partial(kernel, nr, nc),
-        out_shape=(jax.ShapeDtypeStruct((nb, z), f32), jax.ShapeDtypeStruct((8, z), f32)),
-        in_specs=[pl.BlockSpec(memory_space=pltpu.SMEM), vmem, vmem],
-        out_specs=(vmem, vmem),
+        out_shape=(part, part, jax.ShapeDtypeStruct((16, z), f32)),
+        in_specs=[vmem, hbm, hbm],
+        out_specs=(vmem, vmem, vmem),
         scratch_shapes=scratch,
         compiler_params=pltpu.CompilerParams(
-            collective_id=0, has_side_effects=True, vmem_limit_bytes=60 * 1024 * 1024),
-    )(inv, values, sinogram)
-    return sol, res[0]
+            collective_id=0, has_side_effects=True, vmem_limit_bytes=GRANT),
+    )(place, values, sinogram)
+    sol, last = pl.pallas_call(
+        finish_kernel,
+        out_shape=(part, jax.ShapeDtypeStruct((1, z), f32)),
+        in_specs=[vmem, vmem, vmem],
+        out_specs=(hbm, vmem),
+        scratch_shapes=[vmem_of((nb, z), f32), dma((4,))],
+        compiler_params=pltpu.CompilerParams(vmem_limit_bytes=8 * 1024 * 1024),
+    )(sol, step, scale)
+    return sol, last[0]
 
 
 def solution(mesh):

time: 131 us -> 117 us (0.89)
  Pallas kernels: 124 us -> 115 us
  local copies, waits for them, and re-layouts: 3.45 us -> 0 us
    pallas_call x1 -> x2, Pallas kernels: 124 us -> 115 us  [the longest x1 114 us: body(): pl.pallas_call(functools.partial(kernel, nr, nc), out_shape=(part, part,...]
    unnamed x1 -> x0, local copies, waits for them, and re-layouts: 2.26 us -> none
where the time goes in v2:
time: 117 us
  Pallas kernels  115 us (98%)
  between operations  1.45 us (1%)
    pallas_call x1, Pallas kernels, body(): pl.pallas_call(functools.partial(kernel, nr, nc), out_shape=(part, part,...  114 us

profile of v2, /device:TPU:0, one launch (start us, length us, event | category | flops | bytes accessed | tf_op | source)
XLA Modules:
  0.0 117.2 jit_solution(6191238349960976813)
XLA Ops:
  1.3 0.7 compare_select_fusion.place_of
  2.0 113.6 %shard_map.68 = (f32[2048,128]{1,0:T(8,128)S(1)}, f32[2048,128]{1,0:T(8,128)S(1)}, f32[16,128]{1,0:T(8,128)S(1)}) custom-call(s32[1,128]{1,0:T(1,128)S(1)} %compare_select_fusion.place_of, bf16[128,128,128]{2,1,0:T(8,128)(2,1)} %bitcast.6, f32[2048,128]{1,0:T(8,128)} %sino_in.1), custom_call_target="tpu_custom_call" | custom-call | tf_op jit(solution)/shard_map/pallas_call | solution.py:931
  115.5 1.5 %shard_map.69 = (f32[2048,128]{1,0:T(8,128)}, f32[1,128]{1,0:T(1,128)}) custom-call(f32[2048,128]{1,0:T(8,128)S(1)} %get-tuple-element.7.x, f32[2048,128]{1,0:T(8,128)S(1)} %get-tuple-element.8.d, f32[16,128]{1,0:T(8,128)S(1)} %get-tuple-element.9.scale), custom_call_target="tpu_custom_call" | custom-call | tf_op jit(solution)/shard_map/pallas_call | solution.py:940

commit v3 on v2

--- a/solution.py
+++ b/solution.py
@@ -15,7 +15,7 @@
 FINE = 64.0
 LANE = 128
 GRANT = 53000 * 1024
-ORDER = [0, 1] * 10 * ITERS
+ORDER = [int(one) for one in '0001001001001101010110110010010011010101101100100101111101']
 MESH = pl.DeviceIdType.MESH
 
 
@@ -468,8 +468,8 @@
     nr, nc, place_of, tiles_in, sino_in, sol, sdir, res,
     tiles, sino, inv_row, inv,
     fa, ba, y0, yb, bacc, fpart, drecv, xb, vfull, ray, vox, relay, vrow,
-    bsend, brecv, vgat, fsend, frecv, zbuf, cbuf,
-    bs, br, vs, vr, ds_, dr, fs, fr, gs, gr, hs, hr, zs, zr, cs, cr, io,
+    bsend, brecv, vgat, fsend, frecv, zbuf, cbuf, abuf,
+    bs, br, vs, vr, ds_, dr, fs, fr, gs, gr, hs, hr, zs, zr, cs, cr, as_, ar, io,
 ):
     mr = lax.axis_index("row")
     mc = lax.axis_index("col")
@@ -494,10 +494,11 @@
     late = jnp.where(inner, mate, far)
 
     barrier = pltpu.get_barrier_semaphore()
-    for s in range(1, nr):
-        pl.semaphore_signal(barrier, 1, device_id=(lax.rem(mr + s, nr), mc), device_id_type=MESH)
-    for s in range(1, nc):
-        pl.semaphore_signal(barrier, 1, device_id=(mr, lax.rem(mc + s, nc)), device_id_type=MESH)
+    for r in range(nr):
+        for c in range(nc):
+            if r or c:
+                pl.semaphore_signal(
+                    barrier, 1, device_id=(lax.rem(mr + r, nr), lax.rem(mc + c, nc)), device_id_type=MESH)
     load_sino = pltpu.make_async_copy(sino_in, sino, io.at[0])
     load_sino.start()
     load_tiles = []
@@ -563,6 +564,27 @@
             for q in range(1, n):
                 total = total + buf[q]
             return total[:1]
+
+        return finish
+
+    def share_all(vec, h):
+        buf, me = abuf.at[h], mr * nc + mc
+        buf[me] = vec
+        for r in range(nr):
+            for c in range(nc):
+                if r or c:
+                    copy_to(buf.at[me], buf.at[me], as_.at[h], ar.at[h],
+                            lax.rem(mr + r, nr), lax.rem(mc + c, nc)).start()
+        others = buf.at[pl.ds(0, nr * nc - 1)]
+        arrived = copy_to(others, others, as_.at[h], ar.at[h], lax.rem(mr + 1, nr), mc)
+        pending[id(as_), h] = arrived
+
+        def finish():
+            arrived.wait_recv()
+            total = buf[0]
+            for q in range(1, nr * nc):
+                total = total + buf[q]
+            return total
 
         return finish
 
@@ -744,15 +766,15 @@
         beta_of = None
         for k in range(ITERS):
             back_start(k, h)
-            if k == 0 and h:
+            if k == 0 and h == 0:
                 build_ba(mr)
+                build_ba(early)
             yield
             back_relay(k, h)
-            if k == 0:
-                build_ba(cross if h else early)
+            if k == 0 and h == 0:
+                build_ba(cross)
+                build_ba(late)
             yield
-            if k == 0 and h:
-                build_ba(late)
             total = back_sum(k, h)
             if k:
                 betas[k][h] = root(beta_of)
@@ -795,11 +817,9 @@
             raw = raw - wide(column(alpha / beta, h), sr) * ray[k, h]
             n = 2 * k + 2
             if k + 1 == ITERS:
-                beta_of = share_c(row_squares(raw), n, h)
+                beta_of = share_all(row_squares(raw), h)
                 if h:
                     update_dir(k)
-                yield
-                beta_of = share_z(beta_of(), n, h)
                 yield
                 betas[k + 1][h] = root(beta_of)
                 return
@@ -864,7 +884,7 @@
     for load in load_tiles:
         load.wait()
 
-    pl.semaphore_wait(barrier, nr - 1 + nc - 1)
+    pl.semaphore_wait(barrier, nr * nc - 1)
     first_norm = share_z(total, 0, 0)
     halves = [half(0), half(1)]
     for h in ORDER:
@@ -926,7 +946,8 @@
         vmem_of((ITERS, 2, nr, pb, LANE), i16),
         vmem_of((ITERS, 2, nch, pf, LANE), i16), vmem_of((ITERS, 2, nch, pf, LANE), i16),
         vmem_of((norms, 2, nr, 8, z), f32), vmem_of((norms, 2, nc, 8, z), f32),
-    ] + [dma((2, nr))] * 4 + [dma((2, nch))] * 8 + [dma((2, 2))] * 4 + [dma((6,))]
+        vmem_of((2, nr * nc, 1, z), f32),
+    ] + [dma((2, nr))] * 4 + [dma((2, nch))] * 8 + [dma((2, 2))] * 4 + [dma((2,))] * 2 + [dma((6,))]
     part = jax.ShapeDtypeStruct((nb, z), f32)
     sol, step, scale = pl.pallas_call(
         functools.partial(kernel, nr, nc),

time: 117 us -> 108 us (0.923)
  Pallas kernels: 115 us -> 106 us
    pallas_call x1, Pallas kernels: 114 us -> 104 us  [body(): pl.pallas_call(functools.partial(kernel, nr, nc), out_shape=(part, part,...]
where the time goes in v3:
time: 108 us
  Pallas kernels  106 us (98%)
  between operations  1.45 us (1%)
    pallas_call x1, Pallas kernels, body(): pl.pallas_call(functools.partial(kernel, nr, nc), out_shape=(part, part,...  104 us

profile of v3, /device:TPU:0, one launch (start us, length us, event | category | flops | bytes accessed | tf_op | source)
XLA Modules:
  0.0 107.9 jit_solution(5358980150314664053)
XLA Ops:
  1.3 0.7 compare_select_fusion.place_of
  2.0 104.2 %shard_map.68 = (f32[2048,128]{1,0:T(8,128)S(1)}, f32[2048,128]{1,0:T(8,128)S(1)}, f32[16,128]{1,0:T(8,128)S(1)}) custom-call(s32[1,128]{1,0:T(1,128)S(1)} %compare_select_fusion.place_of, bf16[128,128,128]{2,1,0:T(8,128)(2,1)} %bitcast.6, f32[2048,128]{1,0:T(8,128)} %sino_in.1), custom_call_target="tpu_custom_call" | custom-call | tf_op jit(solution)/shard_map/pallas_call | solution.py:952
  106.2 1.5 %shard_map.69 = (f32[2048,128]{1,0:T(8,128)}, f32[1,128]{1,0:T(1,128)}) custom-call(f32[2048,128]{1,0:T(8,128)S(1)} %get-tuple-element.7.x, f32[2048,128]{1,0:T(8,128)S(1)} %get-tuple-element.8.d, f32[16,128]{1,0:T(8,128)S(1)} %get-tuple-element.9.scale), custom_call_target="tpu_custom_call" | custom-call | tf_op jit(solution)/shard_map/pallas_call | solution.py:961

commit v4 on v3

--- a/solution.py
+++ b/solution.py
@@ -15,7 +15,7 @@
 FINE = 64.0
 LANE = 128
 GRANT = 53000 * 1024
-ORDER = [int(one) for one in '0001001001001101010110110010010011010101101100100101111101']
+ORDER = [int(one) for one in '0001001001001011010110110010010010110101101100100101111101']
 MESH = pl.DeviceIdType.MESH
 
 
@@ -768,12 +768,10 @@
             back_start(k, h)
             if k == 0 and h == 0:
                 build_ba(mr)
-                build_ba(early)
             yield
             back_relay(k, h)
             if k == 0 and h == 0:
-                build_ba(cross)
-                build_ba(late)
+                build_ba(early)
             yield
             total = back_sum(k, h)
             if k:
@@ -791,6 +789,9 @@
             alpha_of = share_z(row_squares(raw), 2 * k + 1, h)
             vox_take(k, h, mr)
             fwd_grow(k, h, mr, True)
+            if k == 0 and h == 0:
+                build_ba(cross)
+                build_ba(late)
             if k and h:
                 update_sol(k - 1)
             yield

time: 108 us -> 108 us (level)
  no operation moved by 1% of the time
where the time goes in v4:
time: 108 us; the launch traced here: 107 us
  Pallas kernels  105 us (97%)
  between operations  1.45 us (1%)
    pallas_call x1, Pallas kernels, body(): pl.pallas_call(functools.partial(kernel, nr, nc), out_shape=(part, part,...  104 us

profile of v4, /device:TPU:0, one launch (start us, length us, event | category | flops | bytes accessed | tf_op | source)
XLA Modules:
  0.0 107.5 jit_solution(18078186702448374607)
XLA Ops:
  1.3 0.7 compare_select_fusion.place_of
  2.0 103.8 %shard_map.68 = (f32[2048,128]{1,0:T(8,128)S(1)}, f32[2048,128]{1,0:T(8,128)S(1)}, f32[16,128]{1,0:T(8,128)S(1)}) custom-call(s32[1,128]{1,0:T(1,128)S(1)} %compare_select_fusion.place_of, bf16[128,128,128]{2,1,0:T(8,128)(2,1)} %bitcast.6, f32[2048,128]{1,0:T(8,128)} %sino_in.1), custom_call_target="tpu_custom_call" | custom-call | tf_op jit(solution)/shard_map/pallas_call | solution.py:953
  105.8 1.5 %shard_map.69 = (f32[2048,128]{1,0:T(8,128)}, f32[1,128]{1,0:T(1,128)}) custom-call(f32[2048,128]{1,0:T(8,128)S(1)} %get-tuple-element.7.x, f32[2048,128]{1,0:T(8,128)S(1)} %get-tuple-element.8.d, f32[16,128]{1,0:T(8,128)S(1)} %get-tuple-element.9.scale), custom_call_target="tpu_custom_call" | custom-call | tf_op jit(solution)/shard_map/pallas_call | solution.py:962
